TPU v7x, 32 devices: a whole 2x2x4 slice. The times are simulated.
32 devices in a mesh: zero: 8 (over y, x, core), cols: 4 (over z).
Axes of the slice: x: 2, y: 2, z: 4, core: 2. Of those that a mesh axis runs over, the one named last changes fastest.
Arguments:
- train_gate: bfloat16 [4096, 11008], P('zero', 'cols'), may hold values from -0.125 to 0.125
- low_gate: bfloat16 [4096, 64], P('zero'), may hold values from -0.09375 to 0.09375
- high_gate: bfloat16 [64, 11008], P(None, 'cols'), may hold values from -0.75 to 0.75
- train_up: bfloat16 [4096, 11008], P('zero', 'cols'), may hold values from -0.125 to 0.125
- low_up: bfloat16 [4096, 64], P('zero'), may hold values from -0.09375 to 0.09375
- high_up: bfloat16 [64, 11008], P(None, 'cols'), may hold values from -0.75 to 0.75
- norm_train: float32 [4096], P(('zero', 'cols')), may hold values from 0.25 to 1.75
- norm_step: float32 [4096], P(('zero', 'cols')), may hold values from -0.3 to 0.3
Outputs:
- ready_gate: bfloat16 [4096, 11008], P(None, 'cols')
- ready_up: bfloat16 [4096, 11008], P(None, 'cols')
- factor_gate: float32 [11008], P('cols')
- factor_up: float32 [11008], P('cols')
- serve_norm: bfloat16 [4096], replicated
All inputs are finite; a program needn't handle non-finite values. Where the computation divides by a largest or mean magnitude, that divisor is 1e-20 or more.
Results may differ from a plain program's by a relative error of at most 0.001.
Values may be sent and summed in bfloat16 or wider, within the bound.
A program may use at most 192 MiB of HBM per device.

v0:
```python
import jax
import jax.numpy as jnp
from jax import lax
from jax.sharding import PartitionSpec as P

D_MODEL = 4096
mix_rate = 1.0


def shards(train_gate, low_gate, high_gate, train_up, low_up, high_up, norm_train, norm_step):
    latest_gate = train_gate.astype(jnp.float32) + mix_rate * jnp.dot(
        low_gate, high_gate, preferred_element_type=jnp.float32
    )
    latest_up = train_up.astype(jnp.float32) + mix_rate * jnp.dot(
        low_up, high_up, preferred_element_type=jnp.float32
    )
    total_gate, total_up = lax.psum(
        (jnp.sum(jnp.abs(latest_gate), axis=0), jnp.sum(jnp.abs(latest_up), axis=0)), "zero"
    )
    factor_gate = total_gate / D_MODEL
    factor_up = total_up / D_MODEL
    narrow_gate, narrow_up = (
        (latest_gate / factor_gate).astype(jnp.bfloat16),
        (latest_up / factor_up).astype(jnp.bfloat16),
    )
    ready_gate, ready_up = (
        lax.all_gather(narrow_gate, "zero", axis=0, tiled=True),
        lax.all_gather(narrow_up, "zero", axis=0, tiled=True),
    )
    serve_norm = lax.all_gather(
        (norm_train + norm_step).astype(jnp.bfloat16), ("zero", "cols"), axis=0, tiled=True
    )
    return (ready_gate, ready_up, factor_gate, factor_up, serve_norm)


def solution(mesh):
    return jax.shard_map(
        shards,
        mesh=mesh,
        in_specs=(
            P("zero", "cols"),
            P("zero", None),
            P(None, "cols"),
            P("zero", "cols"),
            P("zero", None),
            P(None, "cols"),
            P(("zero", "cols")),
            P(("zero", "cols")),
        ),
        out_specs=(P(None, "cols"), P(None, "cols"), P("cols"), P("cols"), P()),
        check_vma=False,
    )
```

profile of v0, /device:TPU:0, one launch (start us, length us, event | category | flops | bytes accessed | tf_op | source)
XLA Modules:
  0.0 323.6 jit_solution(7522673026313851749)
XLA Ops:
  7.2 0.0 copy-start
  7.2 0.0 copy-start.3
  7.2 0.0 copy-start.4
  7.2 0.0 all-gather.6.cloned.1.call-start
  7.2 0.9 copy-done
  8.2 0.0 copy-start.5
  8.2 5.4 %abs_reduce_fusion.1 = (f32[2752]{0:T(1024)S(1)}, f32[512,2752]{0,1:T(8,128)}) fusion(bf16[512,64]{0,1:T(8,128)(2,1)} %param.9, bf16[64,2752]{1,0:T(8,128)(2,1)S(1)} %copy-done, bf16[512,2752]{0,1:T(8,128)(2,1)} %param.8), kind=kOutput, calls=%fused_computation.4 | convolution fusion | flops 185988416 | bytes 8882944 | tf_op jit(solution)/shard_map/dot_general | solution.py:11
  13.6 0.0 copy-done.3
  13.6 0.0 copy-done.4
  13.6 0.0 copy-done.5
  13.6 3.5 %abs_reduce_fusion = (f32[2752]{0:T(1024)S(1)}, f32[512,2752]{0,1:T(8,128)}) fusion(bf16[512,64]{0,1:T(8,128)(2,1)S(1)} %copy-done.5, bf16[64,2752]{1,0:T(8,128)(2,1)S(1)} %copy-done.4, bf16[512,2752]{0,1:T(8,128)(2,1)S(1)} %copy-done.3), kind=kOutput, calls=%fused_computation.1 | convolution fusion | flops 185988416 | bytes 8882944 | tf_op jit(solution)/shard_map/dot_general | solution.py:14
  17.2 25.5 %all-reduce = (f32[2752]{0:T(1024)S(1)}, f32[2752]{0:T(1024)S(1)}) all-reduce(f32[2752]{0:T(1024)S(1)} %get-tuple-element.7, f32[2752]{0:T(1024)S(1)} %get-tuple-element.9), channel_id=1, replica_groups=mesh['zero'=8,'cols'=4] {'zero'}, use_global_device_ids=true, to_apply=%region_1.0 | all-reduce | flops 5504 | bytes 44032 | tf_op jit(solution)/shard_map/psum | solution.py:17
  42.7 0.0 copy-start.6
  42.7 4.4 %divide_convert_fusion = bf16[512,2752]{0,1:T(8,128)(2,1)} fusion(f32[512,2752]{0,1:T(8,128)} %get-tuple-element.10, f32[2752]{0:T(1024)S(1)} %broadcast_multiply_fusion), kind=kLoop, calls=%fused_computation | loop fusion | flops 2818048 | bytes 8465152 | tf_op jit(solution)/shard_map/convert_element_type | solution.py:24
  47.1 0.0 all-gather.6.cloned.1.call-update
  47.2 0.0 copy-done.6
  47.2 0.0 all-gather.4.cloned.1.call-start
  47.2 0.0 copy-start.7
  47.2 0.0 copy-start.8
  47.2 0.0 copy-start.9
  47.3 4.4 %divide_convert_fusion.1 = bf16[512,2752]{0,1:T(8,128)(2,1)} fusion(f32[512,2752]{0,1:T(8,128)} %get-tuple-element.8, f32[2752]{0:T(1024)S(1)} %broadcast_multiply_fusion.1), kind=kLoop, calls=%fused_computation.3 | loop fusion | flops 2818048 | bytes 8465152 | tf_op jit(solution)/shard_map/convert_element_type | solution.py:23
  51.6 0.0 all-gather.4.cloned.1.call-update
  51.7 0.0 copy-done.7
  51.7 0.0 copy-done.8
  51.7 0.0 copy-done.9
  51.7 66.0 %all-gather = bf16[32,1,128]{2,1,0:T(2,128)(2,1)S(1)} all-gather(bf16[1,1,128]{2,1,0:T(2,128)(2,1)S(1)} %convert_bitcast_fusion), channel_id=1, replica_groups=mesh['zero'=8,'cols'=4] {'zero','cols'}, dimensions={0}, use_global_device_ids=true | all-gather | bytes 8448 | tf_op jit(solution)/shard_map/all_gather | solution.py:30
  117.7 0.6 reduce
  118.3 47.0 %all-gather.6.cloned.1.call-done = bf16[4096,2752]{0,1:T(8,128)(2,1)} async-done(((bf16[512,2752]{0,1:T(8,128)(2,1)}), bf16[4096,2752]{0,1:T(8,128)(2,1)}) %all-gather.6.cloned.1.call-update) | async-done | bytes 22544400 | tf_op jit(solution)/shard_map/all_gather | solution.py:28
  165.3 121.0 %all-gather.4.cloned.1.call-done = bf16[4096,2752]{0,1:T(8,128)(2,1)} async-done(((bf16[512,2752]{0,1:T(8,128)(2,1)}), bf16[4096,2752]{0,1:T(8,128)(2,1)}) %all-gather.4.cloned.1.call-update) | async-done | bytes 22544400 | tf_op jit(solution)/shard_map/all_gather | solution.py:27
  286.3 0.0 copy-start.2
  286.4 21.1 %copy.15 = bf16[4096,2752]{0,1:T(8,128)(2,1)} copy(bf16[4096,2752]{0,1:T(8,128)(2,1)} %all-gather.4.cloned.1.call-done) | data formatting | bytes 45088768
  307.5 1.2 copy-done.2
  308.7 0.0 copy-start.1
  308.7 8.1 %copy.16 = bf16[4096,2752]{0,1:T(8,128)(2,1)} copy(bf16[4096,2752]{0,1:T(8,128)(2,1)S(1)} %copy-done.2) | data formatting | bytes 45088768
  316.7 0.0 copy-done.1
  (3 shorter events, 0.0 us)
Async XLA Ops:
  7.2 1.0 copy-start
  7.2 6.4 %copy-start.3 = (bf16[512,2752]{0,1:T(8,128)(2,1)S(1)}, bf16[512,2752]{0,1:T(8,128)(2,1)}, u32[]{:S(2)}) copy-start(bf16[512,2752]{0,1:T(8,128)(2,1)} %param.11) | copy-start | bytes 8454148
  7.2 6.4 %copy-start.4 = (bf16[64,2752]{1,0:T(8,128)(2,1)S(1)}, bf16[64,2752]{1,0:T(8,128)(2,1)}, u32[]{:S(2)}) copy-start(bf16[64,2752]{1,0:T(8,128)(2,1)} %param.13) | copy-start | bytes 1056772
  7.2 158.1 %all-gather.6.cloned.1.call-start = ((), (), s32[]{:S(2)}) async-start(), calls=%async_computation.1 | async-start | bytes 25362432 | tf_op jit(solution)/shard_map/all_gather | solution.py:28
  8.2 5.5 %copy-start.5 = (bf16[512,64]{0,1:T(8,128)(2,1)S(1)}, bf16[512,64]{0,1:T(8,128)(2,1)}, u32[]{:S(2)}) copy-start(bf16[512,64]{0,1:T(8,128)(2,1)} %param.12) | copy-start | bytes 196612
  42.7 4.4 %copy-start.6 = (f32[2752]{0:T(1024)}, f32[2752]{0:T(1024)S(1)}, u32[]{:S(2)}) copy-start(f32[2752]{0:T(1024)S(1)} %broadcast_multiply_fusion) | copy-start | bytes 33028
  47.2 239.2 %all-gather.4.cloned.1.call-start = ((), (), s32[]{:S(2)}) async-start(), calls=%async_computation | async-start | bytes 25362432 | tf_op jit(solution)/shard_map/all_gather | solution.py:27
  47.2 4.4 %copy-start.7 = (f32[2752]{0:T(1024)}, f32[2752]{0:T(1024)S(1)}, u32[]{:S(2)}) copy-start(f32[2752]{0:T(1024)S(1)} %broadcast_multiply_fusion.1) | copy-start | bytes 33028
  47.2 4.4 %copy-start.8 = (f32[128]{0:T(128)S(1)}, f32[128]{0:T(128)}, u32[]{:S(2)}) copy-start(f32[128]{0:T(128)} %param.14) | copy-start | bytes 1540
  47.2 4.4 %copy-start.9 = (f32[128]{0:T(128)S(1)}, f32[128]{0:T(128)}, u32[]{:S(2)}) copy-start(f32[128]{0:T(128)} %param.15) | copy-start | bytes 1540
  286.3 22.3 %copy-start.2 = (bf16[4096,2752]{0,1:T(8,128)(2,1)S(1)}, bf16[4096,2752]{0,1:T(8,128)(2,1)}, u32[]{:S(2)}) copy-start(bf16[4096,2752]{0,1:T(8,128)(2,1)} %all-gather.6.cloned.1.call-done) | copy-start | bytes 67633152
  308.7 8.1 %copy-start.1 = (bf16[64,2752]{1,0:T(8,128)(2,1)S(1)}, bf16[64,2752]{1,0:T(8,128)(2,1)}, u32[]{:S(2)}) copy-start(bf16[64,2752]{1,0:T(8,128)(2,1)} %param.10) | copy-start | bytes 1056772
Sparse Core Ops, SparseCore 0:
  47.3 117.9 all-gather.5
  167.8 118.5 all-gather.3
where the time goes:
time: 324 us
  waiting for transfers between devices  168 us (52%)
  blocking collectives  91.5 us (28%)
  local copies, waits for them, and re-layouts  31.3 us (10%)
  between operations  14.1 us (4%)
  other arithmetic  9.46 us (3%)
  matrix products  8.98 us (3%)
    all_gather x1, waiting for transfers between devices, shards(): lax.all_gather(narrow_gate, 'zero', axis=0, tiled=True)  121 us
    all_gather x1, blocking collectives, shards(): lax.all_gather((norm_train + norm_step).astype(jnp.bfloat16), ('zero', 'c...  66 us
    all_gather x1, waiting for transfers between devices, shards(): lax.all_gather(narrow_up, 'zero', axis=0, tiled=True)  47 us
    unnamed x22, local copies, waits for them, and re-layouts  31.3 us
    psum x1, blocking collectives, shards(): lax.psum((jnp.sum(jnp.abs(latest_gate), axis=0), jnp.sum(jnp.abs(latest_u...  25.5 us
  transfers between devices with their start and end apart: 2, of which 2 were waited for; matrix products, arithmetic and copies ran while one was open for 2% of the time, Pallas kernels for 0%

commit v1 on v0

--- a/solution.py
+++ b/solution.py
@@ -23,9 +23,18 @@
         (latest_gate / factor_gate).astype(jnp.bfloat16),
         (latest_up / factor_up).astype(jnp.bfloat16),
     )
+    bring_leaf = lambda here_x: jnp.concatenate(
+        jax.lax.all_to_all(
+            jnp.stack([here_x] * jax.lax.psum(1, axis_name="zero"), 0),
+            axis_name="zero",
+            split_axis=0,
+            concat_axis=0,
+        ),
+        0,
+    )
     ready_gate, ready_up = (
         lax.all_gather(narrow_gate, "zero", axis=0, tiled=True),
-        lax.all_gather(narrow_up, "zero", axis=0, tiled=True),
+        bring_leaf(narrow_up),
     )
     serve_norm = lax.all_gather(
         (norm_train + norm_step).astype(jnp.bfloat16), ("zero", "cols"), axis=0, tiled=True

time: 324 us -> 479 us (1.48)
  waiting for transfers between devices: 168 us -> 256 us
  local copies, waits for them, and re-layouts: 31.3 us -> 88.1 us
  starting transfers between devices: 0.08 us -> 6.56 us
    all_to_all x0 -> x1, waiting for transfers between devices: none -> 256 us  [shards(): jax.lax.all_to_all(jnp.stack([here_x] * jax.lax.psum(1, axis_name='zero')...]
    all_gather x1, waiting for transfers between devices: 121 us -> 0.01 us  [shards(): lax.all_gather(narrow_gate, 'zero', axis=0, tiled=True)]
    all_gather x1 -> x0, waiting for transfers between devices: 47 us -> none  [shards(): lax.all_gather(narrow_up, 'zero', axis=0, tiled=True)]
    all_to_all x0 -> x1, local copies, waits for them, and re-layouts: none -> 29.7 us  [shards(): jax.lax.all_to_all(jnp.stack([here_x] * jax.lax.psum(1, axis_name='zero')...]
    unnamed x22 -> x20, local copies, waits for them, and re-layouts: 31.3 us -> 49 us
    another operation x0 -> x1, local copies, waits for them, and re-layouts: none -> 9.41 us  [shards(): jnp.stack([here_x] * jax.lax.psum(1, axis_name='zero'), 0)]
    all_to_all x0 -> x1, starting transfers between devices: none -> 6.52 us  [shards(): jax.lax.all_to_all(jnp.stack([here_x] * jax.lax.psum(1, axis_name='zero')...]
  transfers between devices with their start and end apart: 2 -> 2, of which waited for: 2 -> 1; matrix products, arithmetic and copies ran while one was open for 2% -> 15% of each run, Pallas kernels for 0% -> 0%
where the time goes in v1:
time: 479 us; the launch traced here: 477 us
  waiting for transfers between devices  256 us (53%)
  blocking collectives  94.6 us (20%)
  local copies, waits for them, and re-layouts  88.1 us (18%)
  between operations  14.1 us (3%)
  matrix products  8.98 us (2%)
  other arithmetic  8.33 us (2%)
  starting transfers between devices  6.56 us (1%)
    all_to_all x1, waiting for transfers between devices, shards(): jax.lax.all_to_all(jnp.stack([here_x] * jax.lax.psum(1, axis_name='zero')...  256 us
    all_gather x1, blocking collectives, shards(): lax.all_gather((norm_train + norm_step).astype(jnp.bfloat16), ('zero', 'c...  69 us
    unnamed x20, local copies, waits for them, and re-layouts  49 us
    all_to_all x1, local copies, waits for them, and re-layouts, shards(): jax.lax.all_to_all(jnp.stack([here_x] * jax.lax.psum(1, axis_name='zero')...  29.7 us
    psum x1, blocking collectives, shards(): lax.psum((jnp.sum(jnp.abs(latest_gate), axis=0), jnp.sum(jnp.abs(latest_u...  25.5 us
  transfers between devices with their start and end apart: 2, of which 1 were waited for; matrix products, arithmetic and copies ran while one was open for 15% of the time, Pallas kernels for 0%

profile of v1, /device:TPU:0, one launch (start us, length us, event | category | flops | bytes accessed | tf_op | source)
XLA Modules:
  0.0 477.0 jit_solution(14344163282903571455)
XLA Ops:
  7.2 0.0 copy-start
  7.2 0.0 copy-start.2
  7.2 0.0 copy-start.3
  7.2 0.0 all-gather.3.cloned.1.call-start
  7.2 0.9 copy-done
  8.2 0.0 copy-start.4
  8.2 5.4 %abs_reduce_fusion.1 = (f32[2752]{0:T(1024)S(1)}, f32[512,2752]{0,1:T(8,128)}) fusion(bf16[512,64]{0,1:T(8,128)(2,1)} %param.9, bf16[64,2752]{1,0:T(8,128)(2,1)S(1)} %copy-done, bf16[512,2752]{0,1:T(8,128)(2,1)} %param.8), kind=kOutput, calls=%fused_computation.4 | convolution fusion | flops 185988416 | bytes 8882944 | tf_op jit(solution)/shard_map/dot_general | solution.py:11
  13.6 0.0 copy-done.2
  13.6 0.0 copy-done.3
  13.6 0.0 copy-done.4
  13.6 3.5 abs_reduce_fusion
  17.2 25.5 %all-reduce = (f32[2752]{0:T(1024)S(1)}, f32[2752]{0:T(1024)S(1)}) all-reduce(f32[2752]{0:T(1024)S(1)} %get-tuple-element.12, f32[2752]{0:T(1024)S(1)} %get-tuple-element.14), channel_id=1, replica_groups=mesh['zero'=8,'cols'=4] {'zero'}, use_global_device_ids=true, to_apply=%region_1.0 | all-reduce | flops 5504 | bytes 44032 | tf_op jit(solution)/shard_map/psum | solution.py:17
  42.7 0.0 copy-start.5
  42.7 4.4 divide_convert_fusion.1
  47.1 0.0 all-gather.3.cloned.1.call-update
  47.1 0.0 copy-done.5
  47.1 0.0 copy-start.6
  47.2 3.3 divide_convert_fusion
  50.4 9.4 %stack.2 = bf16[8,512,2752]{1,2,0:T(8,128)(2,1)} broadcast(bf16[512,2752]{0,1:T(8,128)(2,1)S(1)} %divide_convert_fusion), dimensions={1,2} | broadcast | bytes 25362432 | tf_op jit(solution)/shard_map/stack | solution.py:28
  59.9 0.0 copy-done.6
  59.9 0.0 copy-start.7
  59.9 0.0 copy-start.8
  59.9 6.5 %all-to-all-start = ((bf16[8,512,2752]{1,2,0:T(8,128)(2,1)}), bf16[8,512,2752]{1,2,0:T(8,128)(2,1)}, u32[]{:S(2)}, u32[]{:S(2)}) async-start(bf16[8,512,2752]{1,2,0:T(8,128)(2,1)} %stack.2), calls=%async_computation | async-start | bytes 45088768 | tf_op jit(solution)/shard_map/all_to_all | solution.py:27
  66.4 0.0 copy-done.7
  66.4 0.0 copy-done.8
  66.4 69.0 %all-gather = bf16[32,1,128]{2,1,0:T(2,128)(2,1)S(1)} all-gather(bf16[1,1,128]{2,1,0:T(2,128)(2,1)S(1)} %convert_bitcast_fusion), channel_id=1, replica_groups=mesh['zero'=8,'cols'=4] {'zero','cols'}, dimensions={0}, use_global_device_ids=true | all-gather | bytes 8448 | tf_op jit(solution)/shard_map/all_gather | solution.py:39
  135.4 0.6 reduce
  136.1 256.4 %all-to-all-done = bf16[8,512,2752]{1,2,0:T(8,128)(2,1)} async-done(((bf16[8,512,2752]{1,2,0:T(8,128)(2,1)}), bf16[8,512,2752]{1,2,0:T(8,128)(2,1)}, u32[]{:S(2)}, u32[]{:S(2)}) %all-to-all-start) | async-done | bytes 22544416 | tf_op jit(solution)/shard_map/all_to_all | solution.py:27
  392.5 29.7 %copy.13 = bf16[8,512,2752]{2,1,0:T(8,128)(2,1)} copy(bf16[8,512,2752]{1,2,0:T(8,128)(2,1)} %all-to-all-done) | data formatting | bytes 45088768 | tf_op jit(solution)/shard_map/all_to_all | solution.py:27
  422.2 28.5 %copy.14 = bf16[4096,2752]{0,1:T(8,128)(2,1)} copy(bf16[4096,2752]{1,0:T(8,128)(2,1)} %bitcast.8) | data formatting | bytes 45088768
  450.7 0.0 all-gather.3.cloned.1.call-done
  450.7 0.0 copy-start.1
  450.7 19.5 %copy.16 = bf16[4096,2752]{0,1:T(8,128)(2,1)} copy(bf16[4096,2752]{0,1:T(8,128)(2,1)} %all-gather.3.cloned.1.call-done) | data formatting | bytes 45088768
  470.2 0.0 copy-done.1
  (3 shorter events, 0.0 us)
Async XLA Ops:
  7.2 1.0 copy-start
  7.2 6.4 %copy-start.2 = (bf16[512,2752]{0,1:T(8,128)(2,1)S(1)}, bf16[512,2752]{0,1:T(8,128)(2,1)}, u32[]{:S(2)}) copy-start(bf16[512,2752]{0,1:T(8,128)(2,1)} %param.11) | copy-start | bytes 8454148
  7.2 6.4 %copy-start.3 = (bf16[64,2752]{1,0:T(8,128)(2,1)S(1)}, bf16[64,2752]{1,0:T(8,128)(2,1)}, u32[]{:S(2)}) copy-start(bf16[64,2752]{1,0:T(8,128)(2,1)} %param.13) | copy-start | bytes 1056772
  7.2 443.5 %all-gather.3.cloned.1.call-start = ((), (), s32[]{:S(2)}) async-start(), calls=%async_computation.1 | async-start | bytes 25362432 | tf_op jit(solution)/shard_map/all_gather | solution.py:36
  8.2 5.5 %copy-start.4 = (bf16[512,64]{0,1:T(8,128)(2,1)S(1)}, bf16[512,64]{0,1:T(8,128)(2,1)}, u32[]{:S(2)}) copy-start(bf16[512,64]{0,1:T(8,128)(2,1)} %param.12) | copy-start | bytes 196612
  42.7 4.4 copy-start.5
  47.1 12.7 %copy-start.6 = (f32[2752]{0:T(1024)}, f32[2752]{0:T(1024)S(1)}, u32[]{:S(2)}) copy-start(f32[2752]{0:T(1024)S(1)} %broadcast_multiply_fusion) | copy-start | bytes 33028
  59.9 6.5 %copy-start.7 = (f32[128]{0:T(128)S(1)}, f32[128]{0:T(128)}, u32[]{:S(2)}) copy-start(f32[128]{0:T(128)} %param.14) | copy-start | bytes 1540
  59.9 6.5 %copy-start.8 = (f32[128]{0:T(128)S(1)}, f32[128]{0:T(128)}, u32[]{:S(2)}) copy-start(f32[128]{0:T(128)} %param.15) | copy-start | bytes 1540
  59.9 332.6 %all-to-all-start = ((bf16[8,512,2752]{1,2,0:T(8,128)(2,1)}), bf16[8,512,2752]{1,2,0:T(8,128)(2,1)}, u32[]{:S(2)}, u32[]{:S(2)}) async-start(bf16[8,512,2752]{1,2,0:T(8,128)(2,1)} %stack.2), calls=%async_computation | async-start | bytes 45088768 | tf_op jit(solution)/shard_map/all_to_all | solution.py:27
  450.7 19.5 %copy-start.1 = (bf16[64,2752]{1,0:T(8,128)(2,1)S(1)}, bf16[64,2752]{1,0:T(8,128)(2,1)}, u32[]{:S(2)}) copy-start(bf16[64,2752]{1,0:T(8,128)(2,1)} %param.10) | copy-start | bytes 1056772
Sparse Core Ops, SparseCore 0:
  47.2 291.6 all-gather.2
